TPU v7x, 32 devices: a whole 2x2x4 slice. The times are simulated.
32 devices in a mesh: gx: 4 (over x, core), gy: 2 (over y), gz: 4 (over z).
Axes of the slice: x: 2, y: 2, z: 4, core: 2. Of those that a mesh axis runs over, the one named last changes fastest.
Arguments:
- output_grad: bfloat16 [32768, 1024], P(('gx', 'gy', 'gz')), may hold values from -6 to 6
- entries: int32 [32768, 32], P(('gx', 'gy', 'gz')), may hold values from 0 to 511, as said below
- weights: bfloat16 [32768, 32], P(('gx', 'gy', 'gz')), may hold values from 0.0099487305 to 0.099609375
- hot_blocks: int32 [32, 4], P(('gx', 'gy', 'gz')), may hold values from -1 to 15, as said below
- block_counts: int32 [32], P(('gx', 'gy', 'gz')), may hold values from 2 to 4, as said below
- param: float32 [4, 4, 128, 1024], P('gx', 'gz', 'gy'), may hold values from -6 to 6
- first_moment: float32 [4, 4, 128, 1024], P('gx', 'gz', 'gy'), may hold values from -4 to 4
- second_moment: float32 [4, 4, 128, 1024], P('gx', 'gz', 'gy'), may hold values from 0.05 to 1
Outputs:
- new_param: float32 [4, 4, 128, 1024], P('gx', 'gz', 'gy')
- new_first: float32 [4, 4, 128, 1024], P('gx', 'gz', 'gy')
- new_second: float32 [4, 4, 128, 1024], P('gx', 'gz', 'gy')
Inputs may be any that keep to these rules, and one draw needn't show every extreme that they name: `hot_blocks`: row d lists device d's hot blocks (block b is rows b * 128 to b * 128 + 127 of the table laid out as 2048 rows) in its first block_counts[d] slots and -1 in the others. The listed blocks of one row differ pairwise modulo 4. Among the devices that differ only in their gz index, some value modulo 4 is listed by every one of them. `block_counts`: among the devices that differ only in their gz index, at least one uses all 4 slots. `entries`: an entry e of a token of device d names a used slot: e // 128 < block_counts[d].
All inputs are finite; a program needn't handle non-finite values.
Results may differ from a plain program's by a relative error of at most 0.00034.
Values sent between devices are 32-bit elements; how exact they have to be, the bound alone decides.
A program may use at most 128 MiB of HBM per device.

v0:
```python
import jax
import jax.numpy as jnp
from jax import lax
from jax.sharding import PartitionSpec as P

BLOCK = 128


first_decay = 0.9
second_decay = 0.99
learning_rate = 0.01
adam_epsilon = 1e-08
first_debias = 1.0 / (1.0 - 0.9**10)
second_debias = 1.0 / (1.0 - 0.99**10)


def adam_update(gradient, param, first_moment, second_moment):
    new_first = first_decay * first_moment + (1.0 - first_decay) * gradient
    new_second = second_decay * second_moment + (1.0 - second_decay) * gradient * gradient
    new_param = param - learning_rate * (new_first * first_debias) / (
        jnp.sqrt(new_second * second_debias) + adam_epsilon
    )
    return (new_param, new_first, new_second)


def shards(
    output_grad, entries, weights, hot_blocks, block_counts, param, first_moment, second_moment
):
    line_size = lax.axis_size("gz")
    column_size = lax.axis_size("gx")
    token_count = output_grad.shape[0]
    feature_width = output_grad.shape[1]
    hot_slots = hot_blocks.shape[1]
    listed_blocks = hot_blocks[0]
    slot_index = jnp.arange(hot_slots, dtype=jnp.int32)
    usable = (slot_index < block_counts[0]) & (listed_blocks >= 0)
    safe_blocks = jnp.maximum(listed_blocks, 0)
    slot_bucket = safe_blocks % line_size
    slot_column = safe_blocks // line_size
    entry_slot = entries // BLOCK
    entry_row = entries % BLOCK
    matches = entry_slot[:, :, None] == slot_index
    entry_bucket = jnp.sum(jnp.where(matches, slot_bucket, 0), axis=2)
    entry_kept = jnp.any(matches & usable, axis=2)
    bucket_index = jnp.arange(line_size, dtype=jnp.int32)
    bucket_weighted = jnp.where(
        (entry_bucket[:, :, None] == bucket_index) & entry_kept[:, :, None],
        weights[:, :, None],
        jnp.zeros((), jnp.bfloat16),
    )
    row_index = jnp.arange(BLOCK, dtype=jnp.int32)
    tok_block = 256
    block_total = token_count // tok_block

    def accumulate(step, total):
        start = (step * tok_block).astype(jnp.int32)
        bucket_part = lax.dynamic_slice_in_dim(bucket_weighted, start, tok_block, 0)
        row_part = (
            lax.dynamic_slice_in_dim(entry_row, start, tok_block, 0)[:, :, None] == row_index
        ).astype(jnp.bfloat16)
        grad_part = lax.dynamic_slice_in_dim(output_grad, start, tok_block, 0)
        spread_part = jnp.einsum(
            "tkb,tkr->brt", bucket_part, row_part, preferred_element_type=jnp.float32
        ).astype(jnp.bfloat16)
        return total + jnp.einsum(
            "brt,td->brd", spread_part, grad_part, preferred_element_type=jnp.float32
        )

    partial_value = lax.fori_loop(
        0, block_total, accumulate, jnp.zeros((line_size, BLOCK, feature_width), jnp.float32)
    )
    bucket_hit = (slot_bucket[None, :] == bucket_index[:, None]) & usable[None, :]
    labels = jnp.sum(jnp.where(bucket_hit, slot_column[None, :] + 1, 0), axis=1) - 1
    column_index = jnp.arange(column_size, dtype=jnp.int32)
    received, sources = (
        lax.all_to_all(partial_value, "gz", split_axis=0, concat_axis=0, tiled=True),
        lax.all_to_all(labels.reshape(line_size, 1), "gz", split_axis=0, concat_axis=0, tiled=True),
    )
    selector = (sources[:, 0][None, :] == column_index[:, None]).astype(jnp.float32)
    merged = jnp.einsum(
        "xs,srd->xrd",
        selector,
        received,
        precision=lax.Precision.HIGHEST,
        preferred_element_type=jnp.float32,
    )
    owner_rows = lax.psum_scatter(
        merged.reshape(column_size * BLOCK, feature_width),
        ("gx", "gy"),
        scatter_dimension=0,
        tiled=True,
    )
    gradient = owner_rows.reshape(param.shape)
    return adam_update(gradient, param, first_moment, second_moment)


def solution(mesh):
    placed = (
        P(("gx", "gy", "gz"), None),
        P(("gx", "gy", "gz"), None),
        P(("gx", "gy", "gz"), None),
        P(("gx", "gy", "gz"), None),
        P(("gx", "gy", "gz")),
        P("gx", "gz", "gy", None),
        P("gx", "gz", "gy", None),
        P("gx", "gz", "gy", None),
    )
    return jax.shard_map(
        shards,
        mesh=mesh,
        in_specs=placed,
        out_specs=(P("gx", "gz", "gy", None), P("gx", "gz", "gy", None), P("gx", "gz", "gy", None)),
        check_vma=False,
    )
```

profile of v0, /device:TPU:0, one launch (start us, length us, event | category | flops | bytes accessed | tf_op | source)
XLA Modules:
  0.0 151.1 jit_solution(8513394139388563075)
XLA Ops:
  7.8 0.7 fusion.26
  8.5 0.7 and_bitcast_fusion
  9.1 0.1 select_reduce_fusion.1
  9.3 0.7 copy.41
  9.9 6.3 %all-to-all-start = ((s32[4,1,1]{2,1,0:T(1,128)}), s32[4,1,1]{2,1,0:T(1,128)S(1)}, u32[]{:S(2)}, u32[]{:S(2)}) async-start(s32[4,1,1]{2,1,0:T(1,128)} %copy.41), calls=%async_computation | async-start | bytes 4096 | tf_op jit(solution)/shard_map/all_to_all | solution.py:77
  16.3 0.7 and_select_fusion
  16.9 0.7 bitcast_and_fusion
  17.6 1.0 copy.49
  18.6 1.1 copy.42
  19.7 0.4 add_select_fusion
  20.2 0.2 copy.46
  20.3 0.1 fusion.18
  20.5 0.1 select_reduce_fusion
  20.6 0.3 copy.48
  20.9 0.2 copy.47
  21.1 1.2 fusion.15
  22.2 21.2 %while.14 = (s32[]{:T(128)}, f32[4,128,1024]{2,1,0:T(8,128)}, s32[1024,32]{1,0:T(8,128)S(1)}, bf16[1024,32,4]{1,2,0:T(4,128)(2,1)S(1)}, bf16[1024,1024]{1,0:T(8,...) while((s32[]{:T(128)}, f32[4,128,1024]{2,1,0:T(8,128)}, s32[1024,32]{1,0:T(8,128)S(1)}, ...), condition=%wide.region_4.5_spmd.clone, body=%wide.region_3.4_spmd.clone.sunk | while | flops 279052288 | bytes 5701801 | solution.py:69
  22.3 1.8 %fusion.35 = bf16[4,128,256]{1,0,2:T(4,128)(2,1)S(1)} fusion(s32[256,32]{1,0:T(8,128)S(1)} %constant_dynamic-slice_fusion.2, bf16[1024,32,4]{1,2,0:T(4,128)(2,1)S(1)} %get-tuple-element.202, s32[]{:T(128)S(6)} %select_n.70), kind=kOutput, calls=%fused_computation.6.clone.1 | convolution fusion | flops 9568256 | bytes 655364 | tf_op jit(solution)/shard_map/while/body/eval_jaxpr/tkb,tkr->brt/dot_general | solution.py:62
  24.1 2.9 %select_add_fusion.2 = f32[4,128,1024]{2,1,0:T(8,128)} fusion(f32[4,128,1024]{2,1,0:T(8,128)} %get-tuple-element.191, pred[]{:T(512)S(6)} %compare.12, bf16[1024,1024]{1,0:T(8,128)(2,1)} %get-tuple-element.203, s32[]{:T(128)S(6)} %select_n.70, bf16[4,128,256]{1,0,2:T(4,128)(2,1)S(1)} %fusion.35), kind=kOutput, calls=%fused_computation.3.clone.1 | convolution fusion | flops 269484032 | bytes 4980741 | tf_op jit(solution)/shard_map/while/body/eval_jaxpr/brt,td->brd/dot_general | solution.py:65
  27.0 1.8 %fusion.35 = bf16[4,128,256]{1,0,2:T(4,128)(2,1)S(1)} fusion(s32[256,32]{1,0:T(8,128)S(1)} %constant_dynamic-slice_fusion.2, bf16[1024,32,4]{1,2,0:T(4,128)(2,1)S(1)} %get-tuple-element.202, s32[]{:T(128)S(6)} %select_n.70), kind=kOutput, calls=%fused_computation.6.clone.1 | convolution fusion | flops 9568256 | bytes 655364 | tf_op jit(solution)/shard_map/while/body/eval_jaxpr/tkb,tkr->brt/dot_general | solution.py:62
  28.9 3.6 %select_add_fusion.2 = f32[4,128,1024]{2,1,0:T(8,128)} fusion(f32[4,128,1024]{2,1,0:T(8,128)} %get-tuple-element.191, pred[]{:T(512)S(6)} %compare.12, bf16[1024,1024]{1,0:T(8,128)(2,1)} %get-tuple-element.203, s32[]{:T(128)S(6)} %select_n.70, bf16[4,128,256]{1,0,2:T(4,128)(2,1)S(1)} %fusion.35), kind=kOutput, calls=%fused_computation.3.clone.1 | convolution fusion | flops 269484032 | bytes 4980741 | tf_op jit(solution)/shard_map/while/body/eval_jaxpr/brt,td->brd/dot_general | solution.py:65
  32.5 1.8 %fusion.35 = bf16[4,128,256]{1,0,2:T(4,128)(2,1)S(1)} fusion(s32[256,32]{1,0:T(8,128)S(1)} %constant_dynamic-slice_fusion.2, bf16[1024,32,4]{1,2,0:T(4,128)(2,1)S(1)} %get-tuple-element.202, s32[]{:T(128)S(6)} %select_n.70), kind=kOutput, calls=%fused_computation.6.clone.1 | convolution fusion | flops 9568256 | bytes 655364 | tf_op jit(solution)/shard_map/while/body/eval_jaxpr/tkb,tkr->brt/dot_general | solution.py:62
  34.3 3.6 %select_add_fusion.2 = f32[4,128,1024]{2,1,0:T(8,128)} fusion(f32[4,128,1024]{2,1,0:T(8,128)} %get-tuple-element.191, pred[]{:T(512)S(6)} %compare.12, bf16[1024,1024]{1,0:T(8,128)(2,1)} %get-tuple-element.203, s32[]{:T(128)S(6)} %select_n.70, bf16[4,128,256]{1,0,2:T(4,128)(2,1)S(1)} %fusion.35), kind=kOutput, calls=%fused_computation.3.clone.1 | convolution fusion | flops 269484032 | bytes 4980741 | tf_op jit(solution)/shard_map/while/body/eval_jaxpr/brt,td->brd/dot_general | solution.py:65
  37.9 1.8 %fusion.35 = bf16[4,128,256]{1,0,2:T(4,128)(2,1)S(1)} fusion(s32[256,32]{1,0:T(8,128)S(1)} %constant_dynamic-slice_fusion.2, bf16[1024,32,4]{1,2,0:T(4,128)(2,1)S(1)} %get-tuple-element.202, s32[]{:T(128)S(6)} %select_n.70), kind=kOutput, calls=%fused_computation.6.clone.1 | convolution fusion | flops 9568256 | bytes 655364 | tf_op jit(solution)/shard_map/while/body/eval_jaxpr/tkb,tkr->brt/dot_general | solution.py:62
  39.8 3.6 %select_add_fusion.2 = f32[4,128,1024]{2,1,0:T(8,128)} fusion(f32[4,128,1024]{2,1,0:T(8,128)} %get-tuple-element.191, pred[]{:T(512)S(6)} %compare.12, bf16[1024,1024]{1,0:T(8,128)(2,1)} %get-tuple-element.203, s32[]{:T(128)S(6)} %select_n.70, bf16[4,128,256]{1,0,2:T(4,128)(2,1)S(1)} %fusion.35), kind=kOutput, calls=%fused_computation.3.clone.1 | convolution fusion | flops 269484032 | bytes 4980741 | tf_op jit(solution)/shard_map/while/body/eval_jaxpr/brt,td->brd/dot_general | solution.py:65
  43.4 0.0 all-to-all-done
  43.4 5.1 %all-to-all-start.1 = ((f32[4,128,1024]{2,1,0:T(8,128)}), f32[4,128,1024]{2,1,0:T(8,128)S(1)}, u32[]{:S(2)}, u32[]{:S(2)}) async-start(f32[4,128,1024]{2,1,0:T(8,128)} %get-tuple-element.112), calls=%async_computation.1 | async-start | bytes 4194304 | tf_op jit(solution)/shard_map/all_to_all | solution.py:76
  48.5 0.0 reduce-scatter.2.cloned.1.call-start
  48.5 0.2 reduce
  48.6 47.5 %all-to-all-done.1 = f32[4,128,1024]{2,1,0:T(8,128)S(1)} async-done(((f32[4,128,1024]{2,1,0:T(8,128)}), f32[4,128,1024]{2,1,0:T(8,128)S(1)}, u32[]{:S(2)}, u32[]{:S(2)}) %all-to-all-start.1) | async-done | bytes 2097184 | tf_op jit(solution)/shard_map/all_to_all | solution.py:76
  96.1 3.3 %fusion.12 = f32[4,128,1024]{2,0,1:T(4,128)S(1)} fusion(f32[4,128,1024]{2,1,0:T(8,128)S(1)} %all-to-all-done.1, s32[4]{0:T(128)S(1)} %reduce), kind=kOutput, calls=%fused_computation.14 | convolution fusion | flops 25165840 | bytes 4194320 | tf_op jit(solution)/shard_map/xs,srd->xrd/dot_general | solution.py:80
  99.4 2.6 %copy.51 = f32[4,128,1024]{2,1,0:T(8,128)} copy(f32[4,128,1024]{2,0,1:T(4,128)S(1)} %fusion.12) | data formatting | bytes 4194304 | tf_op jit(solution)/shard_map/xs,srd->xrd/dot_general | solution.py:80
  101.9 0.0 copy-start
  101.9 0.0 copy-start.1
  102.0 0.0 copy-start.2
  102.0 0.0 reduce-scatter.2.cloned.1.call-update
  102.0 40.4 %reduce-scatter.2.cloned.1.call-done = f32[64,1024]{1,0:T(8,128)} async-done(((f32[512,1024]{1,0:T(8,128)}), f32[64,1024]{1,0:T(8,128)}) %reduce-scatter.2.cloned.1.call-update) | async-done | bytes 262160 | tf_op jit(solution)/shard_map/reduce_scatter | solution.py:87
  142.4 0.0 copy-done
  142.4 0.0 copy-done.1
  142.4 0.0 copy-done.2
  142.4 1.9 %divide_subtract_fusion = (f32[1,1,64,1024]{3,2,1,0:T(8,128)}, f32[1,1,64,1024]{3,2,1,0:T(8,128)}, f32[1,1,64,1024]{3,2,1,0:T(8,128)}) fusion(f32[1,1,64,1024]{3,2,1,0:T(8,128)S(1)} %copy-done, f32[64,1024]{1,0:T(8,128)} %reduce-scatter.2.cloned.1.call-done, f32[1,1,64,1024]{3,2,1,0:T(8,128)S(1)} %copy-done.1, f32[1,1,64,1024]{3,2,1,0:T(8,128)S(1)} %copy-done.2), kind=kLoop, calls=%fused_computation.35 | loop fusion | flops 786432 | bytes 1835008 | tf_op jit(solution)/shard_map/sub | solution.py:20
  (6 shorter events, 0.1 us)
Async XLA Ops:
  9.9 33.5 %all-to-all-start = ((s32[4,1,1]{2,1,0:T(1,128)}), s32[4,1,1]{2,1,0:T(1,128)S(1)}, u32[]{:S(2)}, u32[]{:S(2)}) async-start(s32[4,1,1]{2,1,0:T(1,128)} %copy.41), calls=%async_computation | async-start | bytes 4096 | tf_op jit(solution)/shard_map/all_to_all | solution.py:77
  43.4 52.7 %all-to-all-start.1 = ((f32[4,128,1024]{2,1,0:T(8,128)}), f32[4,128,1024]{2,1,0:T(8,128)S(1)}, u32[]{:S(2)}, u32[]{:S(2)}) async-start(f32[4,128,1024]{2,1,0:T(8,128)} %get-tuple-element.112), calls=%async_computation.1 | async-start | bytes 4194304 | tf_op jit(solution)/shard_map/all_to_all | solution.py:76
  48.5 93.9 %reduce-scatter.2.cloned.1.call-start = ((), (), s32[]{:S(2)}) async-start(), calls=%async_computation.3 | async-start | bytes 2359296 | tf_op jit(solution)/shard_map/reduce_scatter | solution.py:87
  101.9 40.4 %copy-start = (f32[1,1,64,1024]{3,2,1,0:T(8,128)S(1)}, f32[1,1,64,1024]{3,2,1,0:T(8,128)}, u32[]{:S(2)}) copy-start(f32[1,1,64,1024]{3,2,1,0:T(8,128)} %param.15) | copy-start | bytes 786436
  101.9 40.4 %copy-start.1 = (f32[1,1,64,1024]{3,2,1,0:T(8,128)S(1)}, f32[1,1,64,1024]{3,2,1,0:T(8,128)}, u32[]{:S(2)}) copy-start(f32[1,1,64,1024]{3,2,1,0:T(8,128)} %param.16) | copy-start | bytes 786436
  102.0 40.4 %copy-start.2 = (f32[1,1,64,1024]{3,2,1,0:T(8,128)S(1)}, f32[1,1,64,1024]{3,2,1,0:T(8,128)}, u32[]{:S(2)}) copy-start(f32[1,1,64,1024]{3,2,1,0:T(8,128)} %param.17) | copy-start | bytes 786436
Sparse Core Ops, SparseCore 0:
  102.1 40.2 reduce-scatter.1
where the time goes:
time: 152 us; the launch traced here: 151 us
  waiting for transfers between devices  87.9 us (58%)
  matrix products  24.3 us (16%)
  between operations  14.7 us (10%)
  starting transfers between devices  11.4 us (8%)
  other arithmetic  6.68 us (4%)
  local copies, waits for them, and re-layouts  6.03 us (4%)
    all_to_all x1, waiting for transfers between devices, shards(): lax.all_to_all(partial_value, 'gz', split_axis=0, concat_axis=0, tiled=True)  47.5 us
    reduce_scatter x1, waiting for transfers between devices, shards(): lax.psum_scatter(merged.reshape(column_size * BLOCK, feature_width), ('gx...  40.4 us
    dot_general x4, matrix products, accumulate(): jnp.einsum('brt,td->brd', spread_part, grad_part, preferred_element_type=...  13.7 us
    dot_general x4, matrix products, accumulate(): jnp.einsum('tkb,tkr->brt', bucket_part, row_part, preferred_element_type=...  7.39 us
    all_to_all x1, starting transfers between devices, shards(): lax.all_to_all(labels.reshape(line_size, 1), 'gz', split_axis=0, concat_a...  6.35 us
    all_to_all x1, starting transfers between devices, shards(): lax.all_to_all(partial_value, 'gz', split_axis=0, concat_axis=0, tiled=True)  5.09 us
    dot_general x1, matrix products, shards(): jnp.einsum('xs,srd->xrd', selector, received, precision=lax.Precision.HIG...  3.25 us
  transfers between devices with their start and end apart: 3, of which 2 were waited for; matrix products, arithmetic and copies ran while one was open for 18% of the time, Pallas kernels for 0%

commit v1 on v0

v1 whole, which is shorter than its diff:
```python
import functools

import jax
import jax.numpy as jnp
from jax import lax
from jax.experimental import pallas as pl
from jax.experimental.pallas import tpu as pltpu
from jax.sharding import PartitionSpec as P

first_decay = 0.9
second_decay = 0.99
learning_rate = 0.01
adam_epsilon = 1e-08
first_debias = 1.0 / (1.0 - 0.9**10)
second_debias = 1.0 / (1.0 - 0.99**10)

MESH = pl.DeviceIdType.MESH
PIECES = 2
AHEAD = 2
LANES = 128


def adam_update(gradient, param, first_moment, second_moment):
    new_first = first_decay * first_moment + (1.0 - first_decay) * gradient
    new_second = second_decay * second_moment + (1.0 - second_decay) * gradient * gradient
    new_param = param - learning_rate * (new_first * first_debias) / (
        jnp.sqrt(new_second * second_debias) + adam_epsilon
    )
    return (new_param, new_first, new_second)


def kernel(
    sizes,
    hot_ref, count_ref, entries_ref, weights_ref, grad_hbm,
    out_ref,
    grad, code_t, weight_t, spread, partial,
    label_own, label_recv,
    a_recv, b1_send, b1_recv, b2_send, b2_recv, merged, c_recv,
    grad_sem, la_send, la_recv, sa_send, sa_recv, s1_send, s1_recv, s2_send, s2_recv,
    sc_send, sc_recv,
):
    gx_size, gy_size, gz_size, block, slots = sizes
    halves = gx_size // 2
    tokens, width = grad_hbm.shape
    piece = width // PIECES
    rows = block // gy_size
    knn = entries_ref.shape[0]
    count = gz_size * PIECES
    gx, gy, gz = lax.axis_index("gx"), lax.axis_index("gy"), lax.axis_index("gz")
    high, low = gx // 2, gx % 2

    def gy_peer(j):
        return {"gy": (gy + j) % gy_size}

    def high_peer(j):
        return {"gx": ((high + j) % halves) * 2 + low}

    pair_peer = {"gx": high * 2 + 1 - low}
    peers = [gy_peer(j) for j in range(1, gy_size)]
    peers += [pair_peer]
    peers += [high_peer(j) for j in range(1, halves)]
    peers += [{"gz": (gz + j) % gz_size} for j in range(1, gz_size)]

    barrier = pltpu.get_barrier_semaphore()
    for peer in peers:
        pl.semaphore_signal(barrier, inc=1, device_id=peer, device_id_type=MESH)
    load = pltpu.make_async_copy(grad_hbm, grad, grad_sem)
    load.start()

    def bucket_at(p):
        if p == gz_size - 1:
            return gz
        upper = (2 * gz) // gz_size
        down = gz_size - 1 - p
        from_top = down - (gz - down + gz_size) // gz_size
        from_bottom = p + (p - gz + gz_size) // gz_size
        return (1 - upper) * from_top + upper * from_bottom

    bases, columns, buckets = [], [], []
    for s in range(slots):
        listed = hot_ref[0, s]
        usable = (s < count_ref[0]) & (listed >= 0)
        safe = jnp.maximum(listed, 0)
        bucket = safe % gz_size
        bases.append(jnp.where(usable, bucket * block, -(2**20)))
        columns.append(jnp.where(usable, safe // gz_size, -1))
        buckets.append(jnp.where(usable, bucket, -1))
    labels = []
    for p in range(gz_size):
        b = bucket_at(p)
        label = jnp.int32(-1)
        for s in range(slots):
            label = jnp.where(buckets[s] == b, columns[s], label)
        labels.append(label)
        label_own[p] = jnp.full((8, LANES), label, jnp.int32)

    entry = entries_ref[...]
    slot, row = entry // block, entry % block
    code = jnp.full(entry.shape, -1, jnp.int32)
    for s in range(slots):
        code = jnp.where(slot == s, bases[s] + row, code)
    code_t[...] = code
    weight_t[...] = weights_ref[...].astype(jnp.float32)

    row_index = lax.broadcasted_iota(jnp.int32, (block, LANES), 0)

    def make_spread(p):
        first_row = bucket_at(p) * block

        def lane_tile(j, carry):
            at = pl.ds(pl.multiple_of(j * LANES, LANES), LANES)
            total = jnp.zeros((block, LANES), jnp.float32)
            for k in range(knn):
                target = code_t[pl.ds(k, 1), at] - first_row
                weight = weight_t[pl.ds(k, 1), at]
                total = total + jnp.where(row_index == target, weight, 0.0)
            spread[:, at] = total.astype(jnp.bfloat16)
            return carry

        lax.fori_loop(0, tokens // LANES, lane_tile, 0)

    sent = []

    def remote(src, dst, send_sem, recv_sem, peer):
        return pltpu.make_async_remote_copy(
            src_ref=src, dst_ref=dst, send_sem=send_sem, recv_sem=recv_sem,
            device_id=peer, device_id_type=MESH,
        )

    def launch(copy):
        copy.start()
        sent.append(copy)

    a_copies, b1_copies, b2_copies = {}, {}, {}

    def stage_a(i):
        p, f = i // PIECES, i % PIECES
        if f == 0:
            make_spread(p)
        if i == 0:
            load.wait()
        partial[i] = jnp.dot(
            spread[...], grad[:, f * piece:(f + 1) * piece], preferred_element_type=jnp.float32
        )
        if i == 0:
            pl.semaphore_wait(barrier, len(peers))
            for j in range(1, gy_size):
                copy = remote(label_own, label_recv.at[j - 1], la_send.at[j - 1],
                              la_recv.at[j - 1], gy_peer(j))
                launch(copy)
                a_copies["label", j] = copy
        for j in range(1, gy_size):
            to = (gy + j) % gy_size
            copy = remote(
                partial.at[i, pl.ds(pl.multiple_of(to * rows, rows), rows), :],
                a_recv.at[i, j - 1], sa_send.at[i, j - 1], sa_recv.at[i, j - 1], gy_peer(j),
            )
            launch(copy)
            a_copies[i, j] = copy

    def column_sum(i, column):
        p = i // PIECES
        mine = partial[i, pl.ds(pl.multiple_of(gy * rows, rows), rows), :]
        total = jnp.where(label_own[p, 0:1, 0:1] == column, mine, 0.0)
        for j in range(1, gy_size):
            total = total + jnp.where(
                label_recv[j - 1, p, 0:1, 0:1] == column, a_recv[i, j - 1], 0.0
            )
        return total

    def stage_b1(i):
        for j in range(1, gy_size):
            if i == 0:
                a_copies["label", j].wait_recv()
            a_copies[i, j].wait_recv()
        for t in range(halves):
            b1_send[i, t] = column_sum(i, ((high + t) % halves) * 2 + 1 - low)
        copy = remote(b1_send.at[i], b1_recv.at[i], s1_send.at[i], s1_recv.at[i], pair_peer)
        launch(copy)
        b1_copies[i] = copy

    def stage_b2(i):
        b1_copies[i].wait_recv()
        for t in range(1, halves):
            b2_send[i, t - 1] = column_sum(i, ((high + t) % halves) * 2 + low) + b1_recv[i, t]
            copy = remote(b2_send.at[i, t - 1], b2_recv.at[i, t - 1], s2_send.at[i, t - 1],
                          s2_recv.at[i, t - 1], high_peer(t))
            launch(copy)
            b2_copies[i, t] = copy
        merged[i] = column_sum(i, high * 2 + low) + b1_recv[i, 0]

    def stage_c(i):
        p, f = i // PIECES, i % PIECES
        for t in range(1, halves):
            b2_copies[i, t].wait_recv()
        total = merged[i]
        for t in range(1, halves):
            total = total + b2_recv[i, t - 1]
        if p < gz_size - 1:
            merged[i] = total
            launch(remote(merged.at[i], c_recv.at[gz, f], sc_send.at[i], sc_recv.at[gz, f],
                          {"gz": bucket_at(p)}))
            return
        for j in range(1, gz_size):
            source = (gz + j) % gz_size
            remote(merged.at[i], c_recv.at[source, f], sc_send.at[i], sc_recv.at[source, f],
                   {"gz": source}).wait_recv()
            total = total + c_recv[source, f]
        out_ref[:, f * piece:(f + 1) * piece] = total

    for i in range(count + AHEAD + 1):
        if 0 <= i - AHEAD < count:
            stage_b1(i - AHEAD)
        if i < count:
            stage_a(i)
        if 0 <= i - AHEAD < count:
            stage_b2(i - AHEAD)
        if 0 <= i - AHEAD - 1 < count:
            stage_c(i - AHEAD - 1)
    for copy in sent:
        copy.wait_send()


def shards(
    output_grad, entries, weights, hot_blocks, block_counts, param, first_moment, second_moment
):
    gx_size, gy_size, gz_size = (lax.axis_size(a) for a in ("gx", "gy", "gz"))
    slots = hot_blocks.shape[1]
    tokens, width = output_grad.shape
    rows = param.shape[2]
    block = rows * gy_size
    knn = entries.shape[1]
    piece = width // PIECES
    count = gz_size * PIECES
    halves = gx_size // 2
    f32 = jnp.float32
    dma = pltpu.SemaphoreType.DMA
    gradient = pl.pallas_call(
        functools.partial(kernel, (gx_size, gy_size, gz_size, block, slots)),
        out_shape=jax.ShapeDtypeStruct((rows, width), f32),
        in_specs=[
            pl.BlockSpec(memory_space=pltpu.SMEM),
            pl.BlockSpec(memory_space=pltpu.SMEM),
            pl.BlockSpec(memory_space=pltpu.VMEM),
            pl.BlockSpec(memory_space=pltpu.VMEM),
            pl.BlockSpec(memory_space=pl.ANY),
        ],
        out_specs=pl.BlockSpec(memory_space=pltpu.VMEM),
        scratch_shapes=[
            pltpu.VMEM((tokens, width), jnp.bfloat16),
            pltpu.VMEM((knn, tokens), jnp.int32),
            pltpu.VMEM((knn, tokens), f32),
            pltpu.VMEM((block, tokens), jnp.bfloat16),
            pltpu.VMEM((count, block, piece), f32),
            pltpu.VMEM((gz_size, 8, LANES), jnp.int32),
            pltpu.VMEM((gy_size - 1, gz_size, 8, LANES), jnp.int32),
            pltpu.VMEM((count, gy_size - 1, rows, piece), f32),
            pltpu.VMEM((count, halves, rows, piece), f32),
            pltpu.VMEM((count, halves, rows, piece), f32),
            pltpu.VMEM((count, halves - 1, rows, piece), f32),
            pltpu.VMEM((count, halves - 1, rows, piece), f32),
            pltpu.VMEM((count, rows, piece), f32),
            pltpu.VMEM((gz_size, PIECES, rows, piece), f32),
            dma,
            dma((gy_size - 1,)),
            dma((gy_size - 1,)),
            dma((count, gy_size - 1)),
            dma((count, gy_size - 1)),
            dma((count,)),
            dma((count,)),
            dma((count, halves - 1)),
            dma((count, halves - 1)),
            dma((count,)),
            dma((gz_size, PIECES)),
        ],
        compiler_params=pltpu.CompilerParams(
            collective_id=0, has_side_effects=True, vmem_limit_bytes=56 * 1024 * 1024
        ),
        cost_estimate=pl.CostEstimate(
            flops=2 * tokens * width * block * gz_size, bytes_accessed=tokens * width * 2,
            transcendentals=0,
        ),
    )(hot_blocks, block_counts, entries.T, weights.T, output_grad)
    return adam_update(gradient.reshape(param.shape), param, first_moment, second_moment)


def solution(mesh):
    tokens = P(("gx", "gy", "gz"), None)
    table = P("gx", "gz", "gy", None)
    placed = (tokens, tokens, tokens, tokens, P(("gx", "gy", "gz")), table, table, table)
    return jax.shard_map(
        shards, mesh=mesh, in_specs=placed, out_specs=(table, table, table), check_vma=False
    )
```

time: 152 us -> 47.1 us (0.31)
  waiting for transfers between devices: 87.9 us -> 0 us
  Pallas kernels: 0 us -> 43.6 us
  matrix products: 24.3 us -> 0 us
  between operations: 14.7 us -> 1.4 us
  starting transfers between devices: 11.4 us -> 0 us
  local copies, waits for them, and re-layouts: 6.03 us -> 0.01 us
  other arithmetic: 6.68 us -> 1.92 us
    all_to_all x2 -> x0, waiting for transfers between devices: 47.5 us -> none  [the longest x1 47.5 us: shards(): lax.all_to_all(partial_value, 'gz', split_axis=0, concat_axis=0, tiled=True)]
    pallas_call x0 -> x1, Pallas kernels: none -> 43.6 us  [shards(): pl.pallas_call(functools.partial(kernel, (gx_size, gy_size, gz_size, bloc...]
    reduce_scatter x1 -> x0, waiting for transfers between devices: 40.4 us -> none  [shards(): lax.psum_scatter(merged.reshape(column_size * BLOCK, feature_width), ('gx...]
    dot_general x9 -> x0, matrix products: 24.3 us -> none  [the longest x4 13.7 us: accumulate(): jnp.einsum('brt,td->brd', spread_part, grad_part, preferred_element_type=...]
    all_to_all x2 -> x0, starting transfers between devices: 11.4 us -> none  [the longest x1 6.35 us: shards(): lax.all_to_all(labels.reshape(line_size, 1), 'gz', split_axis=0, concat_a...]
    dot_general x1 -> x0, local copies, waits for them, and re-layouts: 2.57 us -> none  [shards(): jnp.einsum('xs,srd->xrd', selector, received, precision=lax.Precision.HIG...]
    select_n x3 -> x0, other arithmetic: 2.26 us -> none  [the longest x1 1.15 us: shards(): jnp.where((entry_bucket[:, :, None] == bucket_index) & entry_kept[:, :, N...]
    unnamed x8 -> x6, local copies, waits for them, and re-layouts: 2.12 us -> 0.01 us
  transfers between devices with their start and end apart: 3 -> 0, of which waited for: 2 -> 0; matrix products, arithmetic and copies ran while one was open for 18% -> 0% of each run, Pallas kernels for 0% -> 0%
where the time goes in v1:
time: 47.1 us; the launch traced here: 47 us
  Pallas kernels  43.6 us (93%)
  other arithmetic  1.92 us (4%)
  between operations  1.4 us (3%)
    pallas_call x1, Pallas kernels, shards(): pl.pallas_call(functools.partial(kernel, (gx_size, gy_size, gz_size, bloc...  43.6 us
    sub x1, other arithmetic, adam_update(): param - learning_rate * (new_first * first_debias) / (jnp.sqrt(new_second...  1.92 us

profile of v1, /device:TPU:0, one launch (start us, length us, event | category | flops | bytes accessed | tf_op | source)
XLA Modules:
  0.0 47.0 jit_solution(17355655792623170609)
XLA Ops:
  0.6 0.0 copy-start.2
  0.6 0.0 copy-start.1
  0.7 0.0 copy-start
  1.4 43.6 %shard_map.103 = f32[64,1024]{1,0:T(8,128)} custom-call(s32[1,4]{1,0:T(1,128)} %hot_ref.1, s32[1]{0:T(128)S(6)} %copy.11.count_ref, s32[32,1024]{1,0:T(8,128)} %bitcast.10, bf16[32,1024]{1,0:T(8,128)(2,1)} %bitcast.11, bf16[1024,1024]{1,0:T(8,128)(2,1)} %grad_hbm.1), custom_call_target="tpu_custom_call" | custom-call | flops 1073741824 | bytes 2097152 | tf_op jit(solution)/shard_map/pallas_call | solution.py:238
  45.0 0.0 copy-done.2
  45.0 0.0 copy-done.1
  45.0 0.0 copy-done
  45.0 1.9 %divide_subtract_fusion = (f32[1,1,64,1024]{3,2,1,0:T(8,128)}, f32[1,1,64,1024]{3,2,1,0:T(8,128)}, f32[1,1,64,1024]{3,2,1,0:T(8,128)}) fusion(f32[1,1,64,1024]{3,2,1,0:T(8,128)S(1)} %copy-done, f32[64,1024]{1,0:T(8,128)} %shard_map.103, f32[1,1,64,1024]{3,2,1,0:T(8,128)S(1)} %copy-done.1, f32[1,1,64,1024]{3,2,1,0:T(8,128)S(1)} %copy-done.2), kind=kLoop, calls=%fused_computation.4 | loop fusion | flops 786432 | bytes 1835008 | tf_op jit(solution)/shard_map/sub | solution.py:26
Async XLA Ops:
  0.6 44.4 %copy-start.2 = (f32[1,1,64,1024]{3,2,1,0:T(8,128)S(1)}, f32[1,1,64,1024]{3,2,1,0:T(8,128)}, u32[]{:S(2)}) copy-start(f32[1,1,64,1024]{3,2,1,0:T(8,128)} %param.15) | copy-start | bytes 786436
  0.6 44.4 %copy-start.1 = (f32[1,1,64,1024]{3,2,1,0:T(8,128)S(1)}, f32[1,1,64,1024]{3,2,1,0:T(8,128)}, u32[]{:S(2)}) copy-start(f32[1,1,64,1024]{3,2,1,0:T(8,128)} %param.14) | copy-start | bytes 786436
  0.7 44.4 %copy-start = (f32[1,1,64,1024]{3,2,1,0:T(8,128)S(1)}, f32[1,1,64,1024]{3,2,1,0:T(8,128)}, u32[]{:S(2)}) copy-start(f32[1,1,64,1024]{3,2,1,0:T(8,128)} %param.13) | copy-start | bytes 786436

commit v2 on v1

--- a/solution.py
+++ b/solution.py
@@ -16,7 +16,10 @@
 
 MESH = pl.DeviceIdType.MESH
 PIECES = 2
-AHEAD = 2
+AHEAD = 3
+LATE = PIECES
+PAIR_LAG = 0
+HIGH_LAG = 3
 LANES = 128
 
 
@@ -59,7 +62,7 @@
     peers = [gy_peer(j) for j in range(1, gy_size)]
     peers += [pair_peer]
     peers += [high_peer(j) for j in range(1, halves)]
-    peers += [{"gz": (gz + j) % gz_size} for j in range(1, gz_size)]
+    peers += [{"gz": (gz + 1) % gz_size}, {"gz": (gz + gz_size - 1) % gz_size}]
 
     barrier = pltpu.get_barrier_semaphore()
     for peer in peers:
@@ -189,36 +192,79 @@
             b2_copies[i, t] = copy
         merged[i] = column_sum(i, high * 2 + low) + b1_recv[i, 0]
 
+    from_below = (gz + gz_size - 1) // gz_size
+    from_above = (2 * gz_size - 2 - gz) // gz_size
+
+    def line_copy(i):
+        p, f = i // PIECES, i % PIECES
+        bucket = bucket_at(p)
+        up = (bucket - gz + gz_size) // gz_size
+        copy = remote(merged.at[i], c_recv.at[up, bucket, f], sc_send.at[i],
+                      sc_recv.at[up, bucket, f], {"gz": gz + 2 * up - 1})
+        relays = up * from_below + (1 - up) * from_above
+        return copy, relays, up, bucket, f
+
     def stage_c(i):
-        p, f = i // PIECES, i % PIECES
         for t in range(1, halves):
             b2_copies[i, t].wait_recv()
         total = merged[i]
         for t in range(1, halves):
             total = total + b2_recv[i, t - 1]
-        if p < gz_size - 1:
-            merged[i] = total
-            launch(remote(merged.at[i], c_recv.at[gz, f], sc_send.at[i], sc_recv.at[gz, f],
-                          {"gz": bucket_at(p)}))
+        merged[i] = total
+        if i // PIECES < gz_size - 1:
+            copy, relays = line_copy(i)[:2]
+
+            @pl.when(relays == 0)
+            def _():
+                copy.start()
+
+    def add_arrived(i, direction, bucket, f):
+        remote(merged.at[i], c_recv.at[direction, bucket, f], sc_send.at[i],
+               sc_recv.at[direction, bucket, f], {"gz": (gz + 1) % gz_size}).wait_recv()
+        merged[i] = merged[i] + c_recv[direction, bucket, f]
+
+    def stage_relay(i):
+        f = i % PIECES
+        if i // PIECES < gz_size - 1:
+            copy, relays, up, bucket, _ = line_copy(i)
+
+            @pl.when(relays == 1)
+            def _():
+                add_arrived(i, up, bucket, f)
+                copy.start()
+
             return
-        for j in range(1, gz_size):
-            source = (gz + j) % gz_size
-            remote(merged.at[i], c_recv.at[source, f], sc_send.at[i], sc_recv.at[source, f],
-                   {"gz": source}).wait_recv()
-            total = total + c_recv[source, f]
-        out_ref[:, f * piece:(f + 1) * piece] = total
-
-    for i in range(count + AHEAD + 1):
-        if 0 <= i - AHEAD < count:
-            stage_b1(i - AHEAD)
-        if i < count:
-            stage_a(i)
-        if 0 <= i - AHEAD < count:
-            stage_b2(i - AHEAD)
-        if 0 <= i - AHEAD - 1 < count:
-            stage_c(i - AHEAD - 1)
+
+        @pl.when(from_below == 1)
+        def _():
+            add_arrived(i, 1, gz, f)
+
+        @pl.when(from_above == 1)
+        def _():
+            add_arrived(i, 0, gz, f)
+
+        out_ref[:, f * piece:(f + 1) * piece] = merged[i]
+
+    def relay_step(i):
+        return i + AHEAD + HIGH_LAG + (LATE if i // PIECES < gz_size - 2 else 0)
+
+    for step in range(count + AHEAD + HIGH_LAG + LATE):
+        i = step - AHEAD
+        if 0 <= i < count:
+            stage_b1(i)
+        if step < count:
+            stage_a(step)
+        if 0 <= i - PAIR_LAG < count:
+            stage_b2(i - PAIR_LAG)
+        if 0 <= i - HIGH_LAG < count:
+            stage_c(i - HIGH_LAG)
+        for r in range(count):
+            if relay_step(r) == step:
+                stage_relay(r)
     for copy in sent:
         copy.wait_send()
+    for i in range(count - PIECES):
+        line_copy(i)[0].wait_send()
 
 
 def shards(
@@ -260,7 +306,7 @@
             pltpu.VMEM((count, halves - 1, rows, piece), f32),
             pltpu.VMEM((count, halves - 1, rows, piece), f32),
             pltpu.VMEM((count, rows, piece), f32),
-            pltpu.VMEM((gz_size, PIECES, rows, piece), f32),
+            pltpu.VMEM((2, gz_size, PIECES, rows, piece), f32),
             dma,
             dma((gy_size - 1,)),
             dma((gy_size - 1,)),
@@ -271,7 +317,7 @@
             dma((count, halves - 1)),
             dma((count, halves - 1)),
             dma((count,)),
-            dma((gz_size, PIECES)),
+            dma((2, gz_size, PIECES)),
         ],
         compiler_params=pltpu.CompilerParams(
             collective_id=0, has_side_effects=True, vmem_limit_bytes=56 * 1024 * 1024

time: 47.1 us -> 45.3 us (0.962)
  Pallas kernels: 43.6 us -> 41.8 us
    pallas_call x1, Pallas kernels: 43.6 us -> 41.8 us  [shards(): pl.pallas_call(functools.partial(kernel, (gx_size, gy_size, gz_size, bloc...]
where the time goes in v2:
time: 45.3 us; the launch traced here: 45.1 us
  Pallas kernels  41.8 us (92%)
  other arithmetic  1.92 us (4%)
  between operations  1.4 us (3%)
    pallas_call x1, Pallas kernels, shards(): pl.pallas_call(functools.partial(kernel, (gx_size, gy_size, gz_size, bloc...  41.8 us
    sub x1, other arithmetic, adam_update(): param - learning_rate * (new_first * first_debias) / (jnp.sqrt(new_second...  1.92 us

profile of v2, /device:TPU:0, one launch (start us, length us, event | category | flops | bytes accessed | tf_op | source)
XLA Modules:
  0.0 45.1 jit_solution(9296469154896218591)
XLA Ops:
  0.6 0.0 copy-start.2
  0.6 0.0 copy-start.1
  0.7 0.0 copy-start
  1.4 41.8 %shard_map.103 = f32[64,1024]{1,0:T(8,128)} custom-call(s32[1,4]{1,0:T(1,128)} %hot_ref.1, s32[1]{0:T(128)S(6)} %copy.11.count_ref, s32[32,1024]{1,0:T(8,128)} %bitcast.10, bf16[32,1024]{1,0:T(8,128)(2,1)} %bitcast.11, bf16[1024,1024]{1,0:T(8,128)(2,1)} %grad_hbm.1), custom_call_target="tpu_custom_call" | custom-call | flops 1073741824 | bytes 2097152 | tf_op jit(solution)/shard_map/pallas_call | solution.py:284
  43.2 0.0 copy-done.2
  43.2 0.0 copy-done.1
  43.2 0.0 copy-done
  43.2 1.9 %divide_subtract_fusion = (f32[1,1,64,1024]{3,2,1,0:T(8,128)}, f32[1,1,64,1024]{3,2,1,0:T(8,128)}, f32[1,1,64,1024]{3,2,1,0:T(8,128)}) fusion(f32[1,1,64,1024]{3,2,1,0:T(8,128)S(1)} %copy-done, f32[64,1024]{1,0:T(8,128)} %shard_map.103, f32[1,1,64,1024]{3,2,1,0:T(8,128)S(1)} %copy-done.1, f32[1,1,64,1024]{3,2,1,0:T(8,128)S(1)} %copy-done.2), kind=kLoop, calls=%fused_computation.4 | loop fusion | flops 786432 | bytes 1835008 | tf_op jit(solution)/shard_map/sub | solution.py:29
Async XLA Ops:
  0.6 42.5 %copy-start.2 = (f32[1,1,64,1024]{3,2,1,0:T(8,128)S(1)}, f32[1,1,64,1024]{3,2,1,0:T(8,128)}, u32[]{:S(2)}) copy-start(f32[1,1,64,1024]{3,2,1,0:T(8,128)} %param.15) | copy-start | bytes 786436
  0.6 42.5 %copy-start.1 = (f32[1,1,64,1024]{3,2,1,0:T(8,128)S(1)}, f32[1,1,64,1024]{3,2,1,0:T(8,128)}, u32[]{:S(2)}) copy-start(f32[1,1,64,1024]{3,2,1,0:T(8,128)} %param.14) | copy-start | bytes 786436
  0.7 42.5 %copy-start = (f32[1,1,64,1024]{3,2,1,0:T(8,128)S(1)}, f32[1,1,64,1024]{3,2,1,0:T(8,128)}, u32[]{:S(2)}) copy-start(f32[1,1,64,1024]{3,2,1,0:T(8,128)} %param.13) | copy-start | bytes 786436
